TPU v7x, 32 devices: a whole 2x2x4 slice. The times are simulated.
32 devices in a mesh: dom: 32 (over z, y, x, core).
Axes of the slice: x: 2, y: 2, z: 4, core: 2. Of those that a mesh axis runs over, the one named last changes fastest.
Arguments:
- node_emb: bfloat16 [16384, 64], P('dom'), may hold values from -6 to 6
- hub_emb: bfloat16 [256, 64], replicated, may hold values from -6 to 6
- tile_vals: bfloat16 [4096, 128, 128], P('dom')
- tile_col: int32 [4096], P('dom'), may hold values from 0 to 5
- tile_dest: int32 [4096], P('dom'), may hold values from 0 to 29, as said below
Outputs:
- node_out: float32 [16384, 64], P('dom')
- hub_out: float32 [256, 64], replicated
Inputs may be any that keep to these rules, and one draw needn't show every extreme that they name: tile_dest below 28 names a partition offset from -3 to 3 and a block of that partition; from 28 up it names a hub block. tile_col below 4 names one of the holding partition's own blocks; from 4 up it names a hub block.
All inputs are finite; a program needn't handle non-finite values.
Results may differ from a plain program's by a relative error of at most 0.0003.
Values sent between devices are 32-bit elements.
A program may use at most 64 MiB of HBM per device.

v0:
```python
import jax
import jax.numpy as jnp
from jax import lax
from jax.sharding import PartitionSpec as P

REACH_BITS = 2
LAYERS = 2


def shifted(block, axis, distance):
    devices = range(lax.axis_size(axis))
    route = [((i - distance) % len(devices), i) for i in devices]
    return lax.ppermute(block, axis, route)


def route_partials(spread, farthest):
    overall = spread[farthest]
    for heading in (1, -1):
        for distance in range(1, farthest + 1):
            overall = overall + shifted(
                spread[farthest + heading * distance], "dom", heading * distance
            )
    return overall


def shards(node_emb, hub_emb, tile_vals, tile_col, tile_dest):
    tile_size = tile_vals.shape[1]
    features = node_emb.shape[1]
    dev_rows = node_emb.shape[0]
    own_blocks = dev_rows // tile_size
    hub_rows = hub_emb.shape[0]
    hub_blocks = hub_rows // tile_size
    tile_count = tile_vals.shape[0]
    farthest = 2**REACH_BITS - 1
    slot_count = 2 * farthest + 1
    target_count = slot_count * own_blocks + hub_blocks
    one_hot = (tile_dest[None, :] == jnp.arange(target_count, dtype=jnp.int32)[:, None]).astype(
        jnp.float32
    )
    current_node = node_emb
    current_hub = hub_emb
    node_total = node_emb.astype(jnp.float32)
    hub_total = hub_emb.astype(jnp.float32)
    for layer_index in range(LAYERS):
        sources = jnp.concatenate([current_node, current_hub], 0).reshape(
            own_blocks + hub_blocks, tile_size, features
        )
        picked = jnp.take(sources, tile_col, axis=0)
        products = jnp.einsum("tij,tjd->tid", tile_vals, picked, preferred_element_type=jnp.float32)
        summed = jnp.dot(
            one_hot,
            products.reshape(tile_count, tile_size * features),
            precision=lax.Precision.HIGHEST,
            preferred_element_type=jnp.float32,
        )
        spread = summed[: slot_count * own_blocks].reshape(slot_count, dev_rows, features)
        hub_part = summed[slot_count * own_blocks :].reshape(hub_rows, features)
        hub_sum = lax.psum(hub_part, "dom")
        node_sum = route_partials(spread, farthest)
        node_total = node_total + node_sum
        hub_total = hub_total + hub_sum
        current_node = node_sum.astype(jnp.bfloat16)
        current_hub = hub_sum.astype(jnp.bfloat16)
    return (node_total / float(LAYERS + 1), hub_total / float(LAYERS + 1))


def solution(mesh):
    in_specs = (P("dom", None), P(), P("dom", None, None), P("dom"), P("dom"))
    out_specs = (P("dom", None), P())
    return jax.shard_map(shards, mesh=mesh, in_specs=in_specs, out_specs=out_specs, check_vma=False)
```

profile of v0, /device:TPU:0, one launch (start us, length us, event | category | flops | bytes accessed | tf_op | source)
XLA Modules:
  0.0 331.4 jit_solution(637796549837110401)
XLA Ops:
  7.2 0.7 compare_select_fusion
  7.9 0.7 compare_and_fusion
  8.5 0.9 copy_bitcast_fusion
  9.4 1.0 gather_fusion
  10.4 7.1 %convolution_bitcast_fusion.1 = f32[128,128,64]{1,2,0:T(8,128)} fusion(bf16[128,128,128]{2,1,0:T(8,128)(2,1)} %param.9, bf16[128,128,64]{1,2,0:T(8,128)(2,1)S(1)} %gather_fusion, pred[128]{0:T(512)(128)(4,1)S(1)} %compare_and_fusion), kind=kOutput, calls=%fused_computation.3 | convolution fusion | flops 269484032 | bytes 10485888 | tf_op jit(solution)/shard_map/tij,tjd->tid/dot_general | solution.py:49
  17.5 5.5 %copy.25 = f32[128,128,64]{0,2,1:T(8,128)} copy(f32[128,128,64]{1,2,0:T(8,128)} %convolution_bitcast_fusion.1) | data formatting | bytes 8388608 | tf_op jit(solution)/shard_map/tij,tjd->tid/dot_general | solution.py:49
  22.9 4.6 %fusion.7 = f32[30,8192]{1,0:T(8,128)S(1)} fusion(f32[128,8192]{0,1:T(8,128)} %bitcast.16, s32[128]{0:T(128)S(1)} %copy-done.3), kind=kOutput, calls=%fused_computation.18 | convolution fusion | flops 377491200 | bytes 5177856 | tf_op jit(solution)/shard_map/dot_general | solution.py:50
  27.5 0.1 fusion.14
  27.7 0.2 squeeze.43
  27.8 0.5 collective-permute-start
  28.4 0.2 squeeze.44
  28.5 2.5 collective-permute-start.1
  31.1 0.2 squeeze.45
  31.3 2.4 collective-permute-start.2
  33.7 0.9 squeeze.46
  34.6 3.0 collective-permute-start.3
  37.5 0.9 squeeze.47
  38.4 1.2 collective-permute-start.4
  39.6 0.9 squeeze.48
  40.5 2.4 collective-permute-done
  42.9 0.8 reshape.60
  43.7 0.2 all-reduce.5.cloned.1.call-start
  43.9 0.2 squeeze.42
  44.1 124.6 %all-reduce.3.cloned.1.call-done = f32[256,64]{1,0:T(8,128)} async-done(((f32[256,64]{1,0:T(8,128)}), f32[256,64]{1,0:T(8,128)}) %all-reduce.3.cloned.1.call-update) | async-done | bytes 65552 | tf_op jit(solution)/shard_map/psum | solution.py:58
  168.7 0.9 convert_element_type.15
  169.8 0.1 copy.27
  169.9 1.0 gather_fusion.1
  170.9 7.1 %convolution_bitcast_fusion = f32[128,128,64]{1,2,0:T(8,128)} fusion(bf16[128,128,128]{2,1,0:T(8,128)(2,1)} %param.9, bf16[128,128,64]{1,2,0:T(8,128)(2,1)S(1)} %gather_fusion.1, pred[128]{0:T(512)(128)(4,1)S(1)} %compare_and_fusion), kind=kOutput, calls=%fused_computation.2 | convolution fusion | flops 269484032 | bytes 10485888 | tf_op jit(solution)/shard_map/tij,tjd->tid/dot_general | solution.py:49
  178.0 5.4 %copy.28 = f32[128,128,64]{0,2,1:T(8,128)} copy(f32[128,128,64]{1,2,0:T(8,128)} %convolution_bitcast_fusion) | data formatting | bytes 8388608 | tf_op jit(solution)/shard_map/tij,tjd->tid/dot_general | solution.py:49
  183.4 4.6 %fusion.6 = f32[30,8192]{1,0:T(8,128)S(1)} fusion(f32[128,8192]{0,1:T(8,128)} %bitcast.17, s32[128]{0:T(128)S(1)} %copy-done.3), kind=kOutput, calls=%fused_computation.17 | convolution fusion | flops 377491200 | bytes 5177856 | tf_op jit(solution)/shard_map/dot_general | solution.py:50
  188.1 0.1 fusion.13
  188.2 0.2 squeeze.54
  188.4 3.3 collective-permute-start.10
  191.7 0.8 reshape.63
  192.8 0.2 squeeze.55
  193.0 0.9 squeeze.50
  193.9 1.6 collective-permute-start.6
  195.5 0.9 squeeze.51
  196.4 0.6 collective-permute-start.7
  196.9 0.9 squeeze.52
  197.8 0.9 squeeze.53
  198.7 0.2 squeeze.49
  198.9 0.8 collective-permute-done.10
  199.7 3.6 %collective-permute-start.9 = (f32[512,64]{1,0:T(8,128)}, f32[512,64]{1,0:T(8,128)S(1)}, u32[]{:S(2)}, u32[]{:S(2)}) collective-permute-start(f32[512,64]{1,0:T(8,128)} %squeeze.53), channel_id=1, source_target_pairs={{1,0},{2,1},{3,2},{4,3},{5,4},{6,5},{7,6},{8,7},{9,8},{10,9},{11,1... | collective-permute-start | bytes 393224 | tf_op jit(solution)/shard_map/ppermute | solution.py:13
  203.3 118.6 %all-reduce.5.cloned.1.call-done = f32[256,64]{1,0:T(8,128)} async-done(((f32[256,64]{1,0:T(8,128)}), f32[256,64]{1,0:T(8,128)}) %all-reduce.5.cloned.1.call-update) | async-done | bytes 65552 | tf_op jit(solution)/shard_map/psum | solution.py:58
  321.9 0.9 add_multiply_fusion.1
  322.9 0.7 copy.31
  323.7 0.8 copy.30
  (32 shorter events, 0.7 us)
Async XLA Ops:
  7.2 161.5 %all-reduce.3.cloned.1.call-start = ((), (), s32[]{:S(2)}) async-start(), calls=%async_computation | async-start | bytes 262144 | tf_op jit(solution)/shard_map/psum | solution.py:58
  17.5 5.5 %copy-start.3 = (s32[128]{0:T(128)S(1)}, s32[128]{0:T(128)}, u32[]{:S(2)}) copy-start(s32[128]{0:T(128)} %param.11) | copy-start | bytes 1540
  27.8 15.0 %collective-permute-start = (f32[512,64]{1,0:T(8,128)S(1)}, f32[512,64]{1,0:T(8,128)S(1)}, u32[]{:S(2)}, u32[]{:S(2)}) collective-permute-start(f32[512,64]{1,0:T(8,128)S(1)} %squeeze.43), channel_id=1, source_target_pairs={{31,0},{0,1},{1,2},{2,3},{3,4},{4,5},{5,6},{6,7},{7,8},{8,9},{9,10... | collective-permute-start | bytes 393224 | tf_op jit(solution)/shard_map/ppermute | solution.py:13
  28.5 141.1 %collective-permute-start.1 = (f32[512,64]{1,0:T(8,128)S(1)}, f32[512,64]{1,0:T(8,128)S(1)}, u32[]{:S(2)}, u32[]{:S(2)}) collective-permute-start(f32[512,64]{1,0:T(8,128)S(1)} %squeeze.44), channel_id=1, source_target_pairs={{30,0},{31,1},{0,2},{1,3},{2,4},{3,5},{4,6},{5,7},{6,8},{7,9},{8,1... | collective-permute-start | bytes 393224 | tf_op jit(solution)/shard_map/ppermute | solution.py:13
  31.3 138.4 %collective-permute-start.2 = (f32[512,64]{1,0:T(8,128)S(1)}, f32[512,64]{1,0:T(8,128)S(1)}, u32[]{:S(2)}, u32[]{:S(2)}) collective-permute-start(f32[512,64]{1,0:T(8,128)S(1)} %squeeze.45), channel_id=1, source_target_pairs={{29,0},{30,1},{31,2},{0,3},{1,4},{2,5},{3,6},{4,7},{5,8},{6,9},{7,... | collective-permute-start | bytes 393224 | tf_op jit(solution)/shard_map/ppermute | solution.py:13
  34.6 135.0 %collective-permute-start.3 = (f32[512,64]{1,0:T(8,128)}, f32[512,64]{1,0:T(8,128)S(1)}, u32[]{:S(2)}, u32[]{:S(2)}) collective-permute-start(f32[512,64]{1,0:T(8,128)} %squeeze.46), channel_id=1, source_target_pairs={{1,0},{2,1},{3,2},{4,3},{5,4},{6,5},{7,6},{8,7},{9,8},{10,9},{11,1... | collective-permute-start | bytes 393224 | tf_op jit(solution)/shard_map/ppermute | solution.py:13
  38.4 131.2 %collective-permute-start.4 = (f32[512,64]{1,0:T(8,128)}, f32[512,64]{1,0:T(8,128)S(1)}, u32[]{:S(2)}, u32[]{:S(2)}) collective-permute-start(f32[512,64]{1,0:T(8,128)} %squeeze.47), channel_id=1, source_target_pairs={{2,0},{3,1},{4,2},{5,3},{6,4},{7,5},{8,6},{9,7},{10,8},{11,9},{12,... | collective-permute-start | bytes 393224 | tf_op jit(solution)/shard_map/ppermute | solution.py:13
  42.9 126.8 %collective-permute-start.5 = (f32[512,64]{1,0:T(8,128)}, f32[512,64]{1,0:T(8,128)S(1)}, u32[]{:S(2)}, u32[]{:S(2)}) collective-permute-start(f32[512,64]{1,0:T(8,128)} %squeeze.48), channel_id=1, source_target_pairs={{3,0},{4,1},{5,2},{6,3},{7,4},{8,5},{9,6},{10,7},{11,8},{12,9},{13... | collective-permute-start | bytes 393224 | tf_op jit(solution)/shard_map/ppermute | solution.py:13
  43.7 278.2 %all-reduce.5.cloned.1.call-start = ((), (), s32[]{:S(2)}) async-start(), calls=%async_computation.1 | async-start | bytes 262144 | tf_op jit(solution)/shard_map/psum | solution.py:58
  183.4 9.1 %copy-start.1 = (bf16[512,64]{0,1:T(8,128)(2,1)S(1)}, bf16[512,64]{0,1:T(8,128)(2,1)}, u32[]{:S(2)}) copy-start(bf16[512,64]{0,1:T(8,128)(2,1)} %param.7) | copy-start | bytes 196612
  183.4 9.2 %copy-start.2 = (bf16[256,64]{0,1:T(8,128)(2,1)S(1)}, bf16[256,64]{0,1:T(8,128)(2,1)}, u32[]{:S(2)}) copy-start(bf16[256,64]{0,1:T(8,128)(2,1)} %param.8) | copy-start | bytes 98308
  183.4 138.5 %copy-start = (f32[256,64]{1,0:T(8,128)S(1)}, f32[256,64]{1,0:T(8,128)}, u32[]{:S(2)}) copy-start(f32[256,64]{1,0:T(8,128)} %all-reduce.3.cloned.1.call-done) | copy-start | bytes 196612
  188.4 11.3 %collective-permute-start.10 = (f32[512,64]{1,0:T(8,128)S(1)}, f32[512,64]{1,0:T(8,128)S(1)}, u32[]{:S(2)}, u32[]{:S(2)}) collective-permute-start(f32[512,64]{1,0:T(8,128)S(1)} %squeeze.54), channel_id=1, source_target_pairs={{2,0},{3,1},{4,2},{5,3},{6,4},{7,5},{8,6},{9,7},{10,8},{11,9},{12,... | collective-permute-start | bytes 393224 | tf_op jit(solution)/shard_map/ppermute | solution.py:13
  193.0 130.6 %collective-permute-start.11 = (f32[512,64]{1,0:T(8,128)S(1)}, f32[512,64]{1,0:T(8,128)S(1)}, u32[]{:S(2)}, u32[]{:S(2)}) collective-permute-start(f32[512,64]{1,0:T(8,128)S(1)} %squeeze.55), channel_id=1, source_target_pairs={{3,0},{4,1},{5,2},{6,3},{7,4},{8,5},{9,6},{10,7},{11,8},{12,9},{13... | collective-permute-start | bytes 393224 | tf_op jit(solution)/shard_map/ppermute | solution.py:13
  193.9 129.7 %collective-permute-start.6 = (f32[512,64]{1,0:T(8,128)}, f32[512,64]{1,0:T(8,128)S(1)}, u32[]{:S(2)}, u32[]{:S(2)}) collective-permute-start(f32[512,64]{1,0:T(8,128)} %squeeze.50), channel_id=1, source_target_pairs={{31,0},{0,1},{1,2},{2,3},{3,4},{4,5},{5,6},{6,7},{7,8},{8,9},{9,10... | collective-permute-start | bytes 393224 | tf_op jit(solution)/shard_map/ppermute | solution.py:13
  196.4 127.2 %collective-permute-start.7 = (f32[512,64]{1,0:T(8,128)}, f32[512,64]{1,0:T(8,128)S(1)}, u32[]{:S(2)}, u32[]{:S(2)}) collective-permute-start(f32[512,64]{1,0:T(8,128)} %squeeze.51), channel_id=1, source_target_pairs={{30,0},{31,1},{0,2},{1,3},{2,4},{3,5},{4,6},{5,7},{6,8},{7,9},{8,1... | collective-permute-start | bytes 393224 | tf_op jit(solution)/shard_map/ppermute | solution.py:13
  197.8 125.8 %collective-permute-start.8 = (f32[512,64]{1,0:T(8,128)}, f32[512,64]{1,0:T(8,128)S(1)}, u32[]{:S(2)}, u32[]{:S(2)}) collective-permute-start(f32[512,64]{1,0:T(8,128)} %squeeze.52), channel_id=1, source_target_pairs={{29,0},{30,1},{31,2},{0,3},{1,4},{2,5},{3,6},{4,7},{5,8},{6,9},{7,... | collective-permute-start | bytes 393224 | tf_op jit(solution)/shard_map/ppermute | solution.py:13
  199.7 123.9 %collective-permute-start.9 = (f32[512,64]{1,0:T(8,128)}, f32[512,64]{1,0:T(8,128)S(1)}, u32[]{:S(2)}, u32[]{:S(2)}) collective-permute-start(f32[512,64]{1,0:T(8,128)} %squeeze.53), channel_id=1, source_target_pairs={{1,0},{2,1},{3,2},{4,3},{5,4},{6,5},{7,6},{8,7},{9,8},{10,9},{11,1... | collective-permute-start | bytes 393224 | tf_op jit(solution)/shard_map/ppermute | solution.py:13
Sparse Core Ops, SparseCore 0:
  43.8 124.8 all-reduce.2
  192.7 129.2 all-reduce.4
where the time goes:
time: 332 us; the launch traced here: 331 us
  waiting for transfers between devices  246 us (74%)
  local copies, waits for them, and re-layouts  24.1 us (7%)
  matrix products  23.3 us (7%)
  starting transfers between devices  19 us (6%)
  between operations  14.2 us (4%)
  other arithmetic  4.29 us (1%)
    psum x2, waiting for transfers between devices, shards(): hub_sum = lax.psum(hub_part, 'dom')  243 us
    ppermute x12, starting transfers between devices, shifted(): return lax.ppermute(block, axis, route)  18.7 us
    dot_general x2, matrix products, shards(): jnp.einsum('tij,tjd->tid', tile_vals, picked, preferred_element_type=jnp....  14.1 us
    dot_general x2, local copies, waits for them, and re-layouts, shards(): jnp.einsum('tij,tjd->tid', tile_vals, picked, preferred_element_type=jnp....  10.9 us
    dot_general x2, matrix products, shards(): jnp.dot(one_hot, products.reshape(tile_count, tile_size * features), prec...  9.19 us
    squeeze x12, local copies, waits for them, and re-layouts, route_partials(): spread[farthest + heading * distance]  7.08 us
  transfers between devices with their start and end apart: 14, of which 4 were waited for; matrix products, arithmetic and copies ran while one was open for 3% of the time, Pallas kernels for 0%

commit v1 on v0

--- a/solution.py
+++ b/solution.py
@@ -55,7 +55,10 @@
         )
         spread = summed[: slot_count * own_blocks].reshape(slot_count, dev_rows, features)
         hub_part = summed[slot_count * own_blocks :].reshape(hub_rows, features)
-        hub_sum = lax.psum(hub_part, "dom")
+        devices_2, hub_sum = (lax.axis_size("dom"), hub_part)
+        for reach in [1 << k for k in range(devices_2.bit_length() - 1)]:
+            pairs = [(i_2, i_2 ^ reach) for i_2 in range(devices_2)]
+            hub_sum = hub_sum + lax.ppermute(hub_sum, "dom", pairs)
         node_sum = route_partials(spread, farthest)
         node_total = node_total + node_sum
         hub_total = hub_total + hub_sum

time: 332 us -> 137 us (0.41)
  waiting for transfers between devices: 246 us -> 65.6 us
  between operations: 14.2 us -> 0.87 us
    psum x2 -> x0, waiting for transfers between devices: 243 us -> none  [shards(): hub_sum = lax.psum(hub_part, 'dom')]
    ppermute x0 -> x10, waiting for transfers between devices: none -> 33.5 us  [shards(): hub_sum = hub_sum + lax.ppermute(hub_sum, 'dom', pairs)]
    ppermute x12, waiting for transfers between devices: 3.24 us -> 32 us  [shifted(): return lax.ppermute(block, axis, route)]
    ppermute x0 -> x10, starting transfers between devices: none -> 6.18 us  [shards(): hub_sum = hub_sum + lax.ppermute(hub_sum, 'dom', pairs)]
    ppermute x12, starting transfers between devices: 18.7 us -> 14.5 us  [shifted(): return lax.ppermute(block, axis, route)]
  transfers between devices with their start and end apart: 14 -> 22, of which waited for: 4 -> 14; matrix products, arithmetic and copies ran while one was open for 3% -> 7% of each run, Pallas kernels for 0% -> 0%
where the time goes in v1:
time: 137 us
  waiting for transfers between devices  65.6 us (48%)
  matrix products  23.3 us (17%)
  local copies, waits for them, and re-layouts  23 us (17%)
  starting transfers between devices  20.7 us (15%)
  other arithmetic  3.52 us (3%)
    ppermute x10, waiting for transfers between devices, shards(): hub_sum = hub_sum + lax.ppermute(hub_sum, 'dom', pairs)  33.5 us
    ppermute x12, waiting for transfers between devices, shifted(): return lax.ppermute(block, axis, route)  32 us
    ppermute x12, starting transfers between devices, shifted(): return lax.ppermute(block, axis, route)  14.5 us
    dot_general x2, matrix products, shards(): jnp.einsum('tij,tjd->tid', tile_vals, picked, preferred_element_type=jnp....  14.1 us
    dot_general x2, local copies, waits for them, and re-layouts, shards(): jnp.einsum('tij,tjd->tid', tile_vals, picked, preferred_element_type=jnp....  11 us
    dot_general x2, matrix products, shards(): jnp.dot(one_hot, products.reshape(tile_count, tile_size * features), prec...  9.16 us
    squeeze x12, local copies, waits for them, and re-layouts, route_partials(): spread[farthest + heading * distance]  7.18 us
    ppermute x10, starting transfers between devices, shards(): hub_sum = hub_sum + lax.ppermute(hub_sum, 'dom', pairs)  6.18 us
  transfers between devices with their start and end apart: 22, of which 14 were waited for; matrix products, arithmetic and copies ran while one was open for 7% of the time, Pallas kernels for 0%

profile of v1, /device:TPU:0, one launch (start us, length us, event | category | flops | bytes accessed | tf_op | source)
XLA Modules:
  0.0 136.9 jit_solution(3921920130993210558)
XLA Ops:
  0.6 0.7 compare_select_fusion
  1.3 0.7 compare_and_fusion
  2.0 0.9 copy_bitcast_fusion
  2.8 1.0 gather_fusion
  3.8 7.1 %convolution_bitcast_fusion.1 = f32[128,128,64]{1,2,0:T(8,128)} fusion(bf16[128,128,128]{2,1,0:T(8,128)(2,1)} %param.9, bf16[128,128,64]{1,2,0:T(8,128)(2,1)S(1)} %gather_fusion, pred[128]{0:T(512)(128)(4,1)S(1)} %compare_and_fusion), kind=kOutput, calls=%fused_computation.3 | convolution fusion | flops 269484032 | bytes 10485888 | tf_op jit(solution)/shard_map/tij,tjd->tid/dot_general | solution.py:49
  10.9 5.5 %copy.27 = f32[128,128,64]{0,2,1:T(8,128)} copy(f32[128,128,64]{1,2,0:T(8,128)} %convolution_bitcast_fusion.1) | data formatting | bytes 8388608 | tf_op jit(solution)/shard_map/tij,tjd->tid/dot_general | solution.py:49
  16.4 4.6 %fusion.7 = f32[30,8192]{1,0:T(8,128)S(1)} fusion(f32[128,8192]{0,1:T(8,128)} %bitcast.16, s32[128]{0:T(128)S(1)} %copy-done.3), kind=kOutput, calls=%fused_computation.19 | convolution fusion | flops 377491200 | bytes 5177856 | tf_op jit(solution)/shard_map/dot_general | solution.py:50
  21.1 0.5 collective-permute-start.6
  21.7 1.0 collective-permute-done.6
  22.7 2.9 %collective-permute-start.7 = (f32[256,64]{1,0:T(8,128)S(1)}, f32[256,64]{1,0:T(8,128)S(1)}, u32[]{:S(2)}, u32[]{:S(2)}) collective-permute-start(f32[256,64]{1,0:T(8,128)S(1)} %add.91), channel_id=1, source_target_pairs={{0,2},{1,3},{2,0},{3,1},{4,6},{5,7},{6,4},{7,5},{8,10},{9,11},{10,... | collective-permute-start | bytes 196616 | tf_op jit(solution)/shard_map/ppermute | solution.py:61
  25.7 0.2 squeeze.43
  26.0 3.5 %collective-permute-done.7 = f32[256,64]{1,0:T(8,128)S(1)} collective-permute-done((f32[256,64]{1,0:T(8,128)S(1)}, f32[256,64]{1,0:T(8,128)S(1)}, u32[]{:S(2)}, u32[]{:S(2)}) %collective-permute-start.7) | collective-permute-done | bytes 65568 | tf_op jit(solution)/shard_map/ppermute | solution.py:61
  29.5 1.8 %collective-permute-start.8 = (f32[256,64]{1,0:T(8,128)S(1)}, f32[256,64]{1,0:T(8,128)S(1)}, u32[]{:S(2)}, u32[]{:S(2)}) collective-permute-start(f32[256,64]{1,0:T(8,128)S(1)} %add.92), channel_id=1, source_target_pairs={{0,4},{1,5},{2,6},{3,7},{4,0},{5,1},{6,2},{7,3},{8,12},{9,13},{10,... | collective-permute-start | bytes 196616 | tf_op jit(solution)/shard_map/ppermute | solution.py:61
  31.3 6.0 %collective-permute-done.8 = f32[256,64]{1,0:T(8,128)S(1)} collective-permute-done((f32[256,64]{1,0:T(8,128)S(1)}, f32[256,64]{1,0:T(8,128)S(1)}, u32[]{:S(2)}, u32[]{:S(2)}) %collective-permute-start.8) | collective-permute-done | bytes 65568 | tf_op jit(solution)/shard_map/ppermute | solution.py:61
  37.3 0.7 collective-permute-start.9
  38.2 0.7 collective-permute-start.1
  39.1 0.9 squeeze.46
  40.0 5.3 %collective-permute-start.3 = (f32[512,64]{1,0:T(8,128)}, f32[512,64]{1,0:T(8,128)S(1)}, u32[]{:S(2)}, u32[]{:S(2)}) collective-permute-start(f32[512,64]{1,0:T(8,128)} %squeeze.46), channel_id=1, source_target_pairs={{1,0},{2,1},{3,2},{4,3},{5,4},{6,5},{7,6},{8,7},{9,8},{10,9},{11,1... | collective-permute-start | bytes 393224 | tf_op jit(solution)/shard_map/ppermute | solution.py:13
  45.3 0.9 squeeze.47
  46.2 0.9 squeeze.48
  47.1 0.6 collective-permute-start.4
  47.7 0.5 collective-permute-start.5
  48.4 5.1 %collective-permute-done.1 = f32[512,64]{1,0:T(8,128)S(1)} collective-permute-done((f32[512,64]{1,0:T(8,128)S(1)}, f32[512,64]{1,0:T(8,128)S(1)}, u32[]{:S(2)}, u32[]{:S(2)}) %collective-permute-start.1) | collective-permute-done | bytes 131104 | tf_op jit(solution)/shard_map/ppermute | solution.py:13
  53.5 6.3 %collective-permute-done.4 = f32[512,64]{1,0:T(8,128)S(1)} collective-permute-done((f32[512,64]{1,0:T(8,128)}, f32[512,64]{1,0:T(8,128)S(1)}, u32[]{:S(2)}, u32[]{:S(2)}) %collective-permute-start.4) | collective-permute-done | bytes 131104 | tf_op jit(solution)/shard_map/ppermute | solution.py:13
  59.8 5.0 %collective-permute-done.5 = f32[512,64]{1,0:T(8,128)S(1)} collective-permute-done((f32[512,64]{1,0:T(8,128)}, f32[512,64]{1,0:T(8,128)S(1)}, u32[]{:S(2)}, u32[]{:S(2)}) %collective-permute-start.5) | collective-permute-done | bytes 131104 | tf_op jit(solution)/shard_map/ppermute | solution.py:13
  64.8 5.4 %collective-permute-done.10 = f32[256,64]{1,0:T(8,128)S(1)} collective-permute-done((f32[256,64]{1,0:T(8,128)S(1)}, f32[256,64]{1,0:T(8,128)S(1)}, u32[]{:S(2)}, u32[]{:S(2)}) %collective-permute-start.10) | collective-permute-done | bytes 65568 | tf_op jit(solution)/shard_map/ppermute | solution.py:61
  70.4 1.0 gather_fusion.1
  71.4 7.1 %convolution_bitcast_fusion = f32[128,128,64]{1,2,0:T(8,128)} fusion(bf16[128,128,128]{2,1,0:T(8,128)(2,1)} %param.9, bf16[128,128,64]{1,2,0:T(8,128)(2,1)S(1)} %gather_fusion.1, pred[128]{0:T(512)(128)(4,1)S(1)} %compare_and_fusion), kind=kOutput, calls=%fused_computation.2 | convolution fusion | flops 269484032 | bytes 10485888 | tf_op jit(solution)/shard_map/tij,tjd->tid/dot_general | solution.py:49
  78.4 5.5 %copy.30 = f32[128,128,64]{0,2,1:T(8,128)} copy(f32[128,128,64]{1,2,0:T(8,128)} %convolution_bitcast_fusion) | data formatting | bytes 8388608 | tf_op jit(solution)/shard_map/tij,tjd->tid/dot_general | solution.py:49
  84.0 4.6 %fusion.6 = f32[30,8192]{1,0:T(8,128)S(1)} fusion(f32[128,8192]{0,1:T(8,128)} %bitcast.17, s32[128]{0:T(128)S(1)} %copy-done.3), kind=kOutput, calls=%fused_computation.18 | convolution fusion | flops 377491200 | bytes 5177856 | tf_op jit(solution)/shard_map/dot_general | solution.py:50
  88.8 1.3 collective-permute-done.17
  90.4 0.2 squeeze.50
  90.7 5.8 %collective-permute-done.18 = f32[256,64]{1,0:T(8,128)S(1)} collective-permute-done((f32[256,64]{1,0:T(8,128)S(1)}, f32[256,64]{1,0:T(8,128)S(1)}, u32[]{:S(2)}, u32[]{:S(2)}) %collective-permute-start.18) | collective-permute-done | bytes 65568 | tf_op jit(solution)/shard_map/ppermute | solution.py:61
  96.7 6.1 %collective-permute-done.19 = f32[256,64]{1,0:T(8,128)S(1)} collective-permute-done((f32[256,64]{1,0:T(8,128)S(1)}, f32[256,64]{1,0:T(8,128)S(1)}, u32[]{:S(2)}, u32[]{:S(2)}) %collective-permute-start.19) | collective-permute-done | bytes 65568 | tf_op jit(solution)/shard_map/ppermute | solution.py:61
  102.9 0.9 squeeze.51
  104.0 0.8 collective-permute-start.13
  104.7 0.9 squeeze.53
  105.6 5.8 %collective-permute-start.14 = (f32[512,64]{1,0:T(8,128)}, f32[512,64]{1,0:T(8,128)S(1)}, u32[]{:S(2)}, u32[]{:S(2)}) collective-permute-start(f32[512,64]{1,0:T(8,128)} %squeeze.53), channel_id=1, source_target_pairs={{1,0},{2,1},{3,2},{4,3},{5,4},{6,5},{7,6},{8,7},{9,8},{10,9},{11,1... | collective-permute-start | bytes 393224 | tf_op jit(solution)/shard_map/ppermute | solution.py:13
  111.5 0.9 squeeze.54
  112.3 0.9 squeeze.55
  113.3 0.5 collective-permute-start.16
  114.2 0.9 add.107
  115.2 4.1 %collective-permute-done.12 = f32[512,64]{1,0:T(8,128)S(1)} collective-permute-done((f32[512,64]{1,0:T(8,128)}, f32[512,64]{1,0:T(8,128)S(1)}, u32[]{:S(2)}, u32[]{:S(2)}) %collective-permute-start.12) | collective-permute-done | bytes 131104 | tf_op jit(solution)/shard_map/ppermute | solution.py:13
  119.3 6.4 %collective-permute-done.15 = f32[512,64]{1,0:T(8,128)S(1)} collective-permute-done((f32[512,64]{1,0:T(8,128)}, f32[512,64]{1,0:T(8,128)S(1)}, u32[]{:S(2)}, u32[]{:S(2)}) %collective-permute-start.15) | collective-permute-done | bytes 131104 | tf_op jit(solution)/shard_map/ppermute | solution.py:13
  125.7 5.2 %collective-permute-done.16 = f32[512,64]{1,0:T(8,128)S(1)} collective-permute-done((f32[512,64]{1,0:T(8,128)}, f32[512,64]{1,0:T(8,128)S(1)}, u32[]{:S(2)}, u32[]{:S(2)}) %collective-permute-start.16) | collective-permute-done | bytes 131104 | tf_op jit(solution)/shard_map/ppermute | solution.py:13
  131.0 0.8 copy.32
  131.8 4.3 %collective-permute-done.21 = f32[256,64]{1,0:T(8,128)S(1)} collective-permute-done((f32[256,64]{1,0:T(8,128)S(1)}, f32[256,64]{1,0:T(8,128)S(1)}, u32[]{:S(2)}, u32[]{:S(2)}) %collective-permute-start.21) | collective-permute-done | bytes 65568 | tf_op jit(solution)/shard_map/ppermute | solution.py:61
  136.2 0.7 copy.33
  (54 shorter events, 2.9 us)
Async XLA Ops:
  10.9 5.5 %copy-start.3 = (s32[128]{0:T(128)S(1)}, s32[128]{0:T(128)}, u32[]{:S(2)}) copy-start(s32[128]{0:T(128)} %param.11) | copy-start | bytes 1540
  21.1 1.5 %collective-permute-start.6 = (f32[256,64]{1,0:T(8,128)S(1)}, f32[256,64]{1,0:T(8,128)S(1)}, u32[]{:S(2)}, u32[]{:S(2)}) collective-permute-start(f32[256,64]{1,0:T(8,128)S(1)} %reshape.60), channel_id=1, source_target_pairs={{0,1},{1,0},{2,3},{3,2},{4,5},{5,4},{6,7},{7,6},{8,9},{9,8},{10,11... | collective-permute-start | bytes 196616 | tf_op jit(solution)/shard_map/ppermute | solution.py:61
  22.7 6.8 %collective-permute-start.7 = (f32[256,64]{1,0:T(8,128)S(1)}, f32[256,64]{1,0:T(8,128)S(1)}, u32[]{:S(2)}, u32[]{:S(2)}) collective-permute-start(f32[256,64]{1,0:T(8,128)S(1)} %add.91), channel_id=1, source_target_pairs={{0,2},{1,3},{2,0},{3,1},{4,6},{5,7},{6,4},{7,5},{8,10},{9,11},{10,... | collective-permute-start | bytes 196616 | tf_op jit(solution)/shard_map/ppermute | solution.py:61
  25.9 21.2 %collective-permute-start = (f32[512,64]{1,0:T(8,128)S(1)}, f32[512,64]{1,0:T(8,128)S(1)}, u32[]{:S(2)}, u32[]{:S(2)}) collective-permute-start(f32[512,64]{1,0:T(8,128)S(1)} %squeeze.43), channel_id=1, source_target_pairs={{31,0},{0,1},{1,2},{2,3},{3,4},{4,5},{5,6},{6,7},{7,8},{8,9},{9,10... | collective-permute-start | bytes 393224 | tf_op jit(solution)/shard_map/ppermute | solution.py:13
  29.5 7.8 %collective-permute-start.8 = (f32[256,64]{1,0:T(8,128)S(1)}, f32[256,64]{1,0:T(8,128)S(1)}, u32[]{:S(2)}, u32[]{:S(2)}) collective-permute-start(f32[256,64]{1,0:T(8,128)S(1)} %add.92), channel_id=1, source_target_pairs={{0,4},{1,5},{2,6},{3,7},{4,0},{5,1},{6,2},{7,3},{8,12},{9,13},{10,... | collective-permute-start | bytes 196616 | tf_op jit(solution)/shard_map/ppermute | solution.py:61
  37.3 10.4 %collective-permute-start.9 = (f32[256,64]{1,0:T(8,128)S(1)}, f32[256,64]{1,0:T(8,128)S(1)}, u32[]{:S(2)}, u32[]{:S(2)}) collective-permute-start(f32[256,64]{1,0:T(8,128)S(1)} %add.93), channel_id=1, source_target_pairs={{0,8},{1,9},{2,10},{3,11},{4,12},{5,13},{6,14},{7,15},{8,0},{9,1},... | collective-permute-start | bytes 196616 | tf_op jit(solution)/shard_map/ppermute | solution.py:61
  38.2 15.3 %collective-permute-start.1 = (f32[512,64]{1,0:T(8,128)S(1)}, f32[512,64]{1,0:T(8,128)S(1)}, u32[]{:S(2)}, u32[]{:S(2)}) collective-permute-start(f32[512,64]{1,0:T(8,128)S(1)} %squeeze.44), channel_id=1, source_target_pairs={{30,0},{31,1},{0,2},{1,3},{2,4},{3,5},{4,6},{5,7},{6,8},{7,9},{8,1... | collective-permute-start | bytes 393224 | tf_op jit(solution)/shard_map/ppermute | solution.py:13
  39.1 14.4 %collective-permute-start.2 = (f32[512,64]{1,0:T(8,128)S(1)}, f32[512,64]{1,0:T(8,128)S(1)}, u32[]{:S(2)}, u32[]{:S(2)}) collective-permute-start(f32[512,64]{1,0:T(8,128)S(1)} %squeeze.45), channel_id=1, source_target_pairs={{29,0},{30,1},{31,2},{0,3},{1,4},{2,5},{3,6},{4,7},{5,8},{6,9},{7,... | collective-permute-start | bytes 393224 | tf_op jit(solution)/shard_map/ppermute | solution.py:13
  40.0 13.5 %collective-permute-start.3 = (f32[512,64]{1,0:T(8,128)}, f32[512,64]{1,0:T(8,128)S(1)}, u32[]{:S(2)}, u32[]{:S(2)}) collective-permute-start(f32[512,64]{1,0:T(8,128)} %squeeze.46), channel_id=1, source_target_pairs={{1,0},{2,1},{3,2},{4,3},{5,4},{6,5},{7,6},{8,7},{9,8},{10,9},{11,1... | collective-permute-start | bytes 393224 | tf_op jit(solution)/shard_map/ppermute | solution.py:13
  47.1 12.7 %collective-permute-start.4 = (f32[512,64]{1,0:T(8,128)}, f32[512,64]{1,0:T(8,128)S(1)}, u32[]{:S(2)}, u32[]{:S(2)}) collective-permute-start(f32[512,64]{1,0:T(8,128)} %squeeze.47), channel_id=1, source_target_pairs={{2,0},{3,1},{4,2},{5,3},{6,4},{7,5},{8,6},{9,7},{10,8},{11,9},{12,... | collective-permute-start | bytes 393224 | tf_op jit(solution)/shard_map/ppermute | solution.py:13
  47.7 17.0 %collective-permute-start.5 = (f32[512,64]{1,0:T(8,128)}, f32[512,64]{1,0:T(8,128)S(1)}, u32[]{:S(2)}, u32[]{:S(2)}) collective-permute-start(f32[512,64]{1,0:T(8,128)} %squeeze.48), channel_id=1, source_target_pairs={{3,0},{4,1},{5,2},{6,3},{7,4},{8,5},{9,6},{10,7},{11,8},{12,9},{13... | collective-permute-start | bytes 393224 | tf_op jit(solution)/shard_map/ppermute | solution.py:13
  53.5 16.7 %collective-permute-start.10 = (f32[256,64]{1,0:T(8,128)S(1)}, f32[256,64]{1,0:T(8,128)S(1)}, u32[]{:S(2)}, u32[]{:S(2)}) collective-permute-start(f32[256,64]{1,0:T(8,128)S(1)} %add.94), channel_id=1, source_target_pairs={{0,16},{1,17},{2,18},{3,19},{4,20},{5,21},{6,22},{7,23},{8,24},{9,... | collective-permute-start | bytes 196616 | tf_op jit(solution)/shard_map/ppermute | solution.py:61
  84.0 29.8 %copy-start.2 = (bf16[256,64]{0,1:T(8,128)(2,1)S(1)}, bf16[256,64]{0,1:T(8,128)(2,1)}, u32[]{:S(2)}) copy-start(bf16[256,64]{0,1:T(8,128)(2,1)} %param.8) | copy-start | bytes 98308
  88.5 25.4 %copy-start = (bf16[512,64]{0,1:T(8,128)(2,1)S(1)}, bf16[512,64]{0,1:T(8,128)(2,1)}, u32[]{:S(2)}) copy-start(bf16[512,64]{0,1:T(8,128)(2,1)} %param.7) | copy-start | bytes 196612
  88.7 1.4 %collective-permute-start.17 = (f32[256,64]{1,0:T(8,128)S(1)}, f32[256,64]{1,0:T(8,128)S(1)}, u32[]{:S(2)}, u32[]{:S(2)}) collective-permute-start(f32[256,64]{1,0:T(8,128)S(1)} %reshape.63), channel_id=1, source_target_pairs={{0,1},{1,0},{2,3},{3,2},{4,5},{5,4},{6,7},{7,6},{8,9},{9,8},{10,11... | collective-permute-start | bytes 196616 | tf_op jit(solution)/shard_map/ppermute | solution.py:61
  90.1 6.4 %collective-permute-start.18 = (f32[256,64]{1,0:T(8,128)S(1)}, f32[256,64]{1,0:T(8,128)S(1)}, u32[]{:S(2)}, u32[]{:S(2)}) collective-permute-start(f32[256,64]{1,0:T(8,128)S(1)} %add.104), channel_id=1, source_target_pairs={{0,2},{1,3},{2,0},{3,1},{4,6},{5,7},{6,4},{7,5},{8,10},{9,11},{10,... | collective-permute-start | bytes 196616 | tf_op jit(solution)/shard_map/ppermute | solution.py:61
  90.6 22.7 %collective-permute-start.11 = (f32[512,64]{1,0:T(8,128)S(1)}, f32[512,64]{1,0:T(8,128)S(1)}, u32[]{:S(2)}, u32[]{:S(2)}) collective-permute-start(f32[512,64]{1,0:T(8,128)S(1)} %squeeze.50), channel_id=1, source_target_pairs={{31,0},{0,1},{1,2},{2,3},{3,4},{4,5},{5,6},{6,7},{7,8},{8,9},{9,10... | collective-permute-start | bytes 393224 | tf_op jit(solution)/shard_map/ppermute | solution.py:13
  96.6 6.2 %collective-permute-start.19 = (f32[256,64]{1,0:T(8,128)S(1)}, f32[256,64]{1,0:T(8,128)S(1)}, u32[]{:S(2)}, u32[]{:S(2)}) collective-permute-start(f32[256,64]{1,0:T(8,128)S(1)} %add.105), channel_id=1, source_target_pairs={{0,4},{1,5},{2,6},{3,7},{4,0},{5,1},{6,2},{7,3},{8,12},{9,13},{10,... | collective-permute-start | bytes 196616 | tf_op jit(solution)/shard_map/ppermute | solution.py:61
  102.8 10.5 %collective-permute-start.20 = (f32[256,64]{1,0:T(8,128)S(1)}, f32[256,64]{1,0:T(8,128)S(1)}, u32[]{:S(2)}, u32[]{:S(2)}) collective-permute-start(f32[256,64]{1,0:T(8,128)S(1)} %add.106), channel_id=1, source_target_pairs={{0,8},{1,9},{2,10},{3,11},{4,12},{5,13},{6,14},{7,15},{8,0},{9,1},... | collective-permute-start | bytes 196616 | tf_op jit(solution)/shard_map/ppermute | solution.py:61
  103.8 15.5 %collective-permute-start.12 = (f32[512,64]{1,0:T(8,128)}, f32[512,64]{1,0:T(8,128)S(1)}, u32[]{:S(2)}, u32[]{:S(2)}) collective-permute-start(f32[512,64]{1,0:T(8,128)} %squeeze.51), channel_id=1, source_target_pairs={{30,0},{31,1},{0,2},{1,3},{2,4},{3,5},{4,6},{5,7},{6,8},{7,9},{8,1... | collective-permute-start | bytes 393224 | tf_op jit(solution)/shard_map/ppermute | solution.py:13
  104.0 15.3 %collective-permute-start.13 = (f32[512,64]{1,0:T(8,128)S(1)}, f32[512,64]{1,0:T(8,128)S(1)}, u32[]{:S(2)}, u32[]{:S(2)}) collective-permute-start(f32[512,64]{1,0:T(8,128)S(1)} %squeeze.52), channel_id=1, source_target_pairs={{29,0},{30,1},{31,2},{0,3},{1,4},{2,5},{3,6},{4,7},{5,8},{6,9},{7,... | collective-permute-start | bytes 393224 | tf_op jit(solution)/shard_map/ppermute | solution.py:13
  105.6 13.6 %collective-permute-start.14 = (f32[512,64]{1,0:T(8,128)}, f32[512,64]{1,0:T(8,128)S(1)}, u32[]{:S(2)}, u32[]{:S(2)}) collective-permute-start(f32[512,64]{1,0:T(8,128)} %squeeze.53), channel_id=1, source_target_pairs={{1,0},{2,1},{3,2},{4,3},{5,4},{6,5},{7,6},{8,7},{9,8},{10,9},{11,1... | collective-permute-start | bytes 393224 | tf_op jit(solution)/shard_map/ppermute | solution.py:13
  113.3 12.4 %collective-permute-start.15 = (f32[512,64]{1,0:T(8,128)}, f32[512,64]{1,0:T(8,128)S(1)}, u32[]{:S(2)}, u32[]{:S(2)}) collective-permute-start(f32[512,64]{1,0:T(8,128)} %squeeze.54), channel_id=1, source_target_pairs={{2,0},{3,1},{4,2},{5,3},{6,4},{7,5},{8,6},{9,7},{10,8},{11,9},{12,... | collective-permute-start | bytes 393224 | tf_op jit(solution)/shard_map/ppermute | solution.py:13
  113.3 0.8 copy-start.1
  113.3 17.6 %collective-permute-start.16 = (f32[512,64]{1,0:T(8,128)}, f32[512,64]{1,0:T(8,128)S(1)}, u32[]{:S(2)}, u32[]{:S(2)}) collective-permute-start(f32[512,64]{1,0:T(8,128)} %squeeze.55), channel_id=1, source_target_pairs={{3,0},{4,1},{5,2},{6,3},{7,4},{8,5},{9,6},{10,7},{11,8},{12,9},{13... | collective-permute-start | bytes 393224 | tf_op jit(solution)/shard_map/ppermute | solution.py:13
  119.2 16.9 %collective-permute-start.21 = (f32[256,64]{1,0:T(8,128)S(1)}, f32[256,64]{1,0:T(8,128)S(1)}, u32[]{:S(2)}, u32[]{:S(2)}) collective-permute-start(f32[256,64]{1,0:T(8,128)S(1)} %add.107), channel_id=1, source_target_pairs={{0,16},{1,17},{2,18},{3,19},{4,20},{5,21},{6,22},{7,23},{8,24},{9,... | collective-permute-start | bytes 196616 | tf_op jit(solution)/shard_map/ppermute | solution.py:61
